TPU v7x, 32 devices: a whole 2x2x4 slice. The times are simulated.
32 devices in a mesh: row: 8 (over z, x), col: 4 (over y, core).
Axes of the slice: x: 2, y: 2, z: 4, core: 2. Of those that a mesh axis runs over, the one named last changes fastest.
Arguments:
- gradient: bfloat16 [3072, 14336], P('row', 'col'), may hold values from -0.1875 to 0.1875
- left_factor: float32 [3072, 3072], P('row', 'col'), may hold values from -1 to 11, as said below
- right_factor: float32 [14336, 14336], P('col', 'row'), may hold values from -1 to 3, as said below
- left_basis: bfloat16 [3072, 3072], P('row', 'col'), may hold values from -0.109375 to 0.109375
- right_basis: bfloat16 [14336, 2048], P('row', 'col'), may hold values from -0.046875 to 0.046875
Outputs:
- left_new: float32 [3072, 3072], P('row', 'col')
- right_new: float32 [14336, 14336], P('col', 'row')
- left_out: float32 [3072, 3072], P('row', 'col')
- right_out: float32 [14336, 2048], P('col', 'row')
Inputs may be any that keep to these rules, and one draw needn't show every extreme that they name: left_factor is symmetric. right_factor is symmetric.
All inputs are finite; a program needn't handle non-finite values.
Results may differ from a plain program's by a relative error of at most 0.0029.
Values may be sent and summed in bfloat16 or wider, within the bound.
A program may use at most 192 MiB of HBM per device.

v0:
```python
import jax
import jax.numpy as jnp
from jax import lax
from jax.sharding import PartitionSpec as P

DMODEL = 3072
DHIDDEN = 14336
ema_decay = 0.95
epsilon = 1e-06


def spread(block, axis, holder):
    block = jnp.where(lax.axis_index(axis) == holder, block, jnp.zeros_like(block))
    return lax.psum(block, axis)


def on_device(gradient, left_factor, right_factor, left_basis, right_basis):
    row_count = lax.axis_size("row")
    col_count = lax.axis_size("col")
    row_index = lax.axis_index("row")
    column_slab = lax.all_gather(gradient, "row", axis=0, tiled=True)
    gram_block = lax.psum_scatter(
        lax.dot_general(
            column_slab, gradient, (((1,), (1,)), ((), ())), preferred_element_type=jnp.float32
        ),
        "col",
        scatter_dimension=0,
        tiled=True,
    ).T
    left_new = ema_decay * left_factor + (1.0 - ema_decay) * gram_block
    group_ratio = row_count // col_count
    slab_cols = gradient.shape[1] // group_ratio
    offered = lax.dynamic_slice_in_dim(
        column_slab, row_index % group_ratio * slab_cols, slab_cols, 1
    )
    shared = spread(offered, "col", row_index // group_ratio)
    right_block = lax.dot_general(
        column_slab, shared, (((0,), (0,)), ((), ())), preferred_element_type=jnp.float32
    )
    right_new = ema_decay * right_factor + (1.0 - ema_decay) * right_block
    left_half = left_new.astype(jnp.bfloat16)
    left_rows = lax.all_gather(left_half, "col", axis=1, tiled=True)
    left_prod = jnp.dot(
        left_rows,
        lax.all_gather(left_basis, "row", axis=0, tiled=True),
        preferred_element_type=jnp.float32,
    )
    right_half = right_new.astype(jnp.bfloat16)
    basis_full = lax.all_gather(right_basis, "col", axis=1, tiled=True)
    right_prod = lax.psum_scatter(
        lax.dot_general(
            basis_full, right_half, (((0,), (1,)), ((), ())), preferred_element_type=jnp.float32
        ),
        "row",
        scatter_dimension=0,
        tiled=True,
    ).T
    left_sq = jnp.sum(left_prod * left_prod, axis=0)
    right_sq = jnp.sum(right_prod * right_prod, axis=0)
    left_sq = lax.psum(left_sq, "row")
    right_sq = lax.psum(right_sq, "col")
    left_out = left_prod * lax.rsqrt(left_sq / DMODEL + epsilon)
    right_out = right_prod * lax.rsqrt(right_sq / DHIDDEN + epsilon)
    return (left_new, right_new, left_out, right_out)


def solution(mesh):
    in_specs = (P("row", "col"), P("row", "col"), P("col", "row"), P("row", "col"), P("row", "col"))
    out_specs = (P("row", "col"), P("col", "row"), P("row", "col"), P("col", "row"))
    return jax.shard_map(
        on_device, mesh=mesh, in_specs=in_specs, out_specs=out_specs, check_vma=False
    )
```

profile of v0, /device:TPU:0, one launch (start us, length us, event | category | flops | bytes accessed | tf_op | source)
XLA Modules:
  0.0 1338.3 jit_solution(2984441622477216147)
XLA Ops:
  7.2 0.0 all-gather.5.cloned.1.call-start
  7.2 0.7 all-gather.5.cloned.1.call-update
  7.9 0.0 all-reduce.2.cloned.1.call-start
  8.0 425.7 %all-gather.5.cloned.1.call-done = bf16[3072,3584]{1,0:T(8,128)(2,1)} async-done(((bf16[384,3584]{1,0:T(8,128)(2,1)}), bf16[3072,3584]{1,0:T(8,128)(2,1)}) %all-gather.5.cloned.1.call-update) | async-done | bytes 22020112 | tf_op jit(solution)/shard_map/all_gather | solution.py:21
  433.6 10.6 dynamic-slice_select_fusion
  444.3 0.0 copy-start
  444.3 0.0 all-reduce.2.cloned.1.call-update
  444.3 0.0 reduce-scatter.3.cloned.1.call-start
  444.3 1.7 copy-done
  446.0 17.8 %fusion.2 = f32[3072,384]{1,0:T(8,128)} fusion(bf16[3072,3584]{1,0:T(8,128)(2,1)} %all-gather.5.cloned.1.call-done, bf16[384,3584]{1,0:T(8,128)(2,1)S(1)} %copy-done), kind=kOutput, calls=%fused_computation.12 | convolution fusion | flops 8455716864 | bytes 29491200 | tf_op jit(solution)/shard_map/dot_general | solution.py:23
  463.8 0.0 copy-start.1
  463.8 0.0 reduce-scatter.3.cloned.1.call-update
  463.8 0.0 all-gather.11.cloned.1.call-start
  463.9 0.5 all-gather.11.cloned.1.call-update
  464.4 0.0 all-gather.9.cloned.1.call-start
  464.5 0.5 all-gather.9.cloned.1.call-update
  465.0 0.0 all-gather.7.cloned.1.call-start
  465.0 0.1 copy-done.1
  465.1 0.4 copy.9
  465.5 27.4 %copy.10 = f32[3584,1792]{0,1:T(8,128)} copy(f32[3584,1792]{1,0:T(8,128)} %param.7) | data formatting | bytes 51380224 | tf_op args[2]
  492.9 146.8 %all-reduce.2.cloned.1.call-done = bf16[3072,1792]{1,0:T(8,128)(2,1)} async-done(((bf16[3072,1792]{1,0:T(8,128)(2,1)}), bf16[3072,1792]{1,0:T(8,128)(2,1)}) %all-reduce.2.cloned.1.call-update) | async-done | bytes 11010064 | tf_op jit(solution)/shard_map/psum | solution.py:14
  639.7 50.6 %bitcast_add_fusion = f32[3584,1792]{0,1:T(8,128)} fusion(f32[3584,1792]{0,1:T(8,128)} %copy.10, bf16[3072,1792]{1,0:T(8,128)(2,1)} %all-reduce.2.cloned.1.call-done, bf16[3072,3584]{1,0:T(8,128)(2,1)} %all-gather.5.cloned.1.call-done), kind=kOutput, calls=%fused_computation | convolution fusion | flops 39479279616 | bytes 84410368 | tf_op jit(solution)/shard_map/dot_general | solution.py:37
  690.3 0.1 reduce-scatter.3.cloned.1.call-done
  690.4 2.3 fusion.1
  692.7 0.0 all-gather.7.cloned.1.call-update
  692.7 0.2 reduce-scatter.5.cloned.1.call-start
  692.9 51.2 %all-gather.11.cloned.1.call-done = bf16[1792,2048]{1,0:T(8,128)(2,1)} async-done(((bf16[1792,512]{1,0:T(8,128)(2,1)}), bf16[1792,2048]{1,0:T(8,128)(2,1)}) %all-gather.11.cloned.1.call-update) | async-done | bytes 7340048 | tf_op jit(solution)/shard_map/all_gather | solution.py:49
  744.2 35.4 %convolution_bitcast_fusion = f32[2048,3584]{0,1:T(8,128)} fusion(bf16[1792,2048]{1,0:T(8,128)(2,1)} %all-gather.11.cloned.1.call-done, f32[3584,1792]{0,1:T(8,128)} %bitcast_add_fusion), kind=kOutput, calls=%fused_computation.1 | convolution fusion | flops 26313097216 | bytes 62390272 | tf_op jit(solution)/shard_map/dot_general | solution.py:51
  779.6 0.0 reduce-scatter.5.cloned.1.call-update
  779.6 27.5 %copy.12 = f32[3584,1792]{1,0:T(8,128)} copy(f32[3584,1792]{0,1:T(8,128)} %bitcast_add_fusion) | data formatting | bytes 51380224
  807.1 1.4 copy.11
  808.4 17.1 %all-gather.9.cloned.1.call-done = bf16[3072,768]{1,0:T(8,128)(2,1)} async-done(((bf16[384,768]{1,0:T(8,128)(2,1)}), bf16[3072,768]{1,0:T(8,128)(2,1)}) %all-gather.9.cloned.1.call-update) | async-done | bytes 4718608 | tf_op jit(solution)/shard_map/all_gather | solution.py:45
  825.5 24.4 %all-gather.7.cloned.1.call-done = bf16[384,3072]{0,1:T(8,128)(2,1)} async-done(((bf16[384,768]{0,1:T(8,128)(2,1)}), bf16[384,3072]{0,1:T(8,128)(2,1)}) %all-gather.7.cloned.1.call-update) | async-done | bytes 2359312 | tf_op jit(solution)/shard_map/all_gather | solution.py:42
  850.0 5.1 multiply_reduce_fusion.1
  855.1 22.3 %psum.22 = f32[768]{0:T(1024)S(1)} all-reduce(f32[768]{0:T(1024)S(1)} %get-tuple-element.10), channel_id=1, replica_groups=mesh['row'=8,'col'=4] {'row'}, use_global_device_ids=true, to_apply=%region_3.4 | all-reduce | flops 768 | bytes 6144 | tf_op jit(solution)/shard_map/psum | solution.py:60
  877.4 1.1 broadcast_multiply_fusion
  878.5 439.8 %reduce-scatter.5.cloned.1.call-done = f32[256,3584]{0,1:T(8,128)} async-done(((f32[2048,3584]{0,1:T(8,128)}), f32[256,3584]{0,1:T(8,128)}) %reduce-scatter.5.cloned.1.call-update) | async-done | bytes 3670032 | tf_op jit(solution)/shard_map/reduce_scatter | solution.py:50
  1318.3 2.5 multiply_reduce_fusion
  1320.9 6.5 psum.23
  1327.4 4.1 multiply_bitcast_fusion
  (2 shorter events, 0.0 us)
Async XLA Ops:
  7.2 426.5 %all-gather.5.cloned.1.call-start = ((), (), s32[]{:S(2)}) async-start(), calls=%async_computation.2 | async-start | bytes 24772608 | tf_op jit(solution)/shard_map/all_gather | solution.py:21
  7.9 631.8 %all-reduce.2.cloned.1.call-start = ((), (), s32[]{:S(2)}) async-start(), calls=%async_computation.4 | async-start | bytes 22020096 | tf_op jit(solution)/shard_map/psum | solution.py:14
  444.3 1.8 copy-start
  444.3 246.1 %reduce-scatter.3.cloned.1.call-start = ((), (), s32[]{:S(2)}) async-start(), calls=%async_computation.3 | async-start | bytes 5898240 | tf_op jit(solution)/shard_map/reduce_scatter | solution.py:22
  463.8 1.3 copy-start.1
  463.8 280.3 %all-gather.11.cloned.1.call-start = ((), (), s32[]{:S(2)}) async-start(), calls=%async_computation.7 | async-start | bytes 9175040 | tf_op jit(solution)/shard_map/all_gather | solution.py:49
  464.4 361.1 %all-gather.9.cloned.1.call-start = ((), (), s32[]{:S(2)}) async-start(), calls=%async_computation.6 | async-start | bytes 5308416 | tf_op jit(solution)/shard_map/all_gather | solution.py:45
  465.0 385.0 %all-gather.7.cloned.1.call-start = ((), (), s32[]{:S(2)}) async-start(), calls=%async_computation.5 | async-start | bytes 2949120 | tf_op jit(solution)/shard_map/all_gather | solution.py:42
  692.7 625.6 %reduce-scatter.5.cloned.1.call-start = ((), (), s32[]{:S(2)}) async-start(), calls=%async_computation.8 | async-start | bytes 33030144 | tf_op jit(solution)/shard_map/reduce_scatter | solution.py:50
Sparse Core Ops, SparseCore 0:
  9.5 424.0 all-gather.4
  444.4 195.1 all-reduce.1
  642.2 48.1 reduce-scatter.2
  691.8 52.2 all-gather.10
  746.2 79.3 all-gather.8
  827.5 22.4 all-gather.6
  853.9 464.4 reduce-scatter.4
where the time goes:
time: 1340 us
  waiting for transfers between devices  1110 us (83%)
  matrix products  109 us (8%)
  local copies, waits for them, and re-layouts  58.4 us (4%)
  blocking collectives  28.8 us (2%)
  other arithmetic  20.7 us (2%)
  between operations  14.2 us (1%)
    reduce_scatter x1, waiting for transfers between devices, on_device(): lax.psum_scatter(lax.dot_general(basis_full, right_half, (((0,), (1,)), (...  440 us
    all_gather x1, waiting for transfers between devices, on_device(): column_slab = lax.all_gather(gradient, 'row', axis=0, tiled=True)  426 us
    psum x1, waiting for transfers between devices, spread(): return lax.psum(block, axis)  147 us
    unnamed x8, local copies, waits for them, and re-layouts  58.4 us
    all_gather x1, waiting for transfers between devices, on_device(): basis_full = lax.all_gather(right_basis, 'col', axis=1, tiled=True)  51.2 us
    dot_general x1, matrix products, on_device(): lax.dot_general(column_slab, shared, (((0,), (0,)), ((), ())), preferred_...  50.6 us
    dot_general x1, matrix products, on_device(): lax.dot_general(basis_full, right_half, (((0,), (1,)), ((), ())), preferr...  35.4 us
  transfers between devices with their start and end apart: 7, of which 7 were waited for; matrix products, arithmetic and copies ran while one was open for 13% of the time, Pallas kernels for 0%

commit v1 on v0

--- a/solution.py
+++ b/solution.py
@@ -7,11 +7,14 @@
 DHIDDEN = 14336
 ema_decay = 0.95
 epsilon = 1e-06
+_touch_threads = lambda dev_axis, my_data: jnp.sum(
+    lax.all_gather(my_data, axis_name=dev_axis), axis=0
+)
 
 
 def spread(block, axis, holder):
     block = jnp.where(lax.axis_index(axis) == holder, block, jnp.zeros_like(block))
-    return lax.psum(block, axis)
+    return _touch_threads(axis, block)
 
 
 def on_device(gradient, left_factor, right_factor, left_basis, right_basis):

time: 1340 us -> 1410 us (1.052)
  waiting for transfers between devices: 1110 us -> 1160 us
  other arithmetic: 20.7 us -> 44.5 us
    all_gather x0 -> x1, waiting for transfers between devices: none -> 261 us  [lax.all_gather(my_data, axis_name=dev_axis)]
    psum x1 -> x0, waiting for transfers between devices: 147 us -> none  [spread(): return lax.psum(block, axis)]
    all_gather x1, waiting for transfers between devices: 51.2 us -> 0.01 us  [on_device(): basis_full = lax.all_gather(right_basis, 'col', axis=1, tiled=True)]
    reduce_scatter x1, waiting for transfers between devices: 440 us -> 412 us  [on_device(): lax.psum_scatter(lax.dot_general(basis_full, right_half, (((0,), (1,)), (...]
    reduce_sum x0 -> x1, other arithmetic: none -> 23.6 us  [jnp.sum(lax.all_gather(my_data, axis_name=dev_axis), axis=0)]
    unnamed x8 -> x6, local copies, waits for them, and re-layouts: 58.4 us -> 56.3 us
  transfers between devices with their start and end apart: 7 -> 7, of which waited for: 7 -> 6; matrix products, arithmetic and copies ran while one was open for 13% -> 13% of each run, Pallas kernels for 0% -> 0%
where the time goes in v1:
time: 1410 us
  waiting for transfers between devices  1160 us (82%)
  matrix products  110 us (8%)
  local copies, waits for them, and re-layouts  56.3 us (4%)
  other arithmetic  44.5 us (3%)
  blocking collectives  28.8 us (2%)
  between operations  14.2 us (1%)
    all_gather x1, waiting for transfers between devices, on_device(): column_slab = lax.all_gather(gradient, 'row', axis=0, tiled=True)  426 us
    reduce_scatter x1, waiting for transfers between devices, on_device(): lax.psum_scatter(lax.dot_general(basis_full, right_half, (((0,), (1,)), (...  412 us
    all_gather x1, waiting for transfers between devices, lax.all_gather(my_data, axis_name=dev_axis)  261 us
    unnamed x6, local copies, waits for them, and re-layouts  56.3 us
    dot_general x1, matrix products, on_device(): lax.dot_general(column_slab, shared, (((0,), (0,)), ((), ())), preferred_...  50.7 us
    dot_general x1, matrix products, on_device(): lax.dot_general(basis_full, right_half, (((0,), (1,)), ((), ())), preferr...  35.8 us
  transfers between devices with their start and end apart: 7, of which 6 were waited for; matrix products, arithmetic and copies ran while one was open for 13% of the time, Pallas kernels for 0%

profile of v1, /device:TPU:0, one launch (start us, length us, event | category | flops | bytes accessed | tf_op | source)
XLA Modules:
  0.0 1411.5 jit_solution(7311706112952049943)
XLA Ops:
  7.2 0.0 all-gather.7.cloned.1.call-start
  7.2 0.7 all-gather.7.cloned.1.call-update
  7.9 0.0 reduce-scatter.3.cloned.1.call-start
  7.9 425.7 %all-gather.7.cloned.1.call-done = bf16[3072,3584]{1,0:T(8,128)(2,1)} async-done(((bf16[384,3584]{1,0:T(8,128)(2,1)}), bf16[3072,3584]{1,0:T(8,128)(2,1)}) %all-gather.7.cloned.1.call-update) | async-done | bytes 22020112 | tf_op jit(solution)/shard_map/all_gather | solution.py:24
  433.6 18.1 %fusion.2 = f32[3072,384]{1,0:T(8,128)} fusion(bf16[3072,3584]{1,0:T(8,128)(2,1)} %all-gather.7.cloned.1.call-done, bf16[384,3584]{1,0:T(8,128)(2,1)} %param.5), kind=kOutput, calls=%fused_computation.12 | convolution fusion | flops 8455716864 | bytes 29491200 | tf_op jit(solution)/shard_map/dot_general | solution.py:26
  451.8 0.0 reduce-scatter.3.cloned.1.call-update
  451.8 0.0 all-gather.15.cloned.1.call-start
  451.9 10.9 dynamic-slice_select_fusion
  462.8 0.0 all-gather.15.cloned.1.call-update
  462.8 0.0 all-gather.13.cloned.1.call-start
  462.9 0.5 all-gather.13.cloned.1.call-update
  463.4 0.0 all-gather.11.cloned.1.call-start
  463.4 0.5 all-gather.11.cloned.1.call-update
  464.0 0.0 copy-start
  464.0 0.0 all-gather.9.cloned.1.call-start
  464.0 27.2 %copy.10 = f32[3584,1792]{0,1:T(8,128)} copy(f32[3584,1792]{1,0:T(8,128)} %param.7) | data formatting | bytes 51380224 | tf_op args[2]
  491.2 0.0 copy-done
  491.2 0.4 copy.9
  491.6 8.3 reduce-scatter.3.cloned.1.call-done
  499.9 2.3 fusion.1
  502.2 0.0 all-gather.9.cloned.1.call-update
  502.2 0.2 reduce-scatter.5.cloned.1.call-start
  502.4 261.1 %all-gather.15.cloned.1.call-done = bf16[12288,1792]{1,0:T(8,128)(2,1)} async-done(((bf16[3072,1792]{1,0:T(8,128)(2,1)}), bf16[12288,1792]{1,0:T(8,128)(2,1)}) %all-gather.15.cloned.1.call-update) | async-done | bytes 44040208 | tf_op jit(solution)/shard_map/all_gather | solution.py:11
  763.5 23.6 %reduce_sum.30 = bf16[3072,1792]{1,0:T(8,128)(2,1)} reduce(bf16[4,3072,1792]{2,1,0:T(8,128)(2,1)} %bitcast.17, bf16[]{:T(256)} %constant.53.clone.1), dimensions={0}, to_apply=%region_1.2 | reduce | flops 16515072 | bytes 55050240 | tf_op jit(solution)/shard_map/reduce_sum | solution.py:10
  787.1 50.7 %bitcast_add_fusion = f32[3584,1792]{0,1:T(8,128)} fusion(f32[3584,1792]{0,1:T(8,128)} %copy.10, bf16[3072,1792]{1,0:T(8,128)(2,1)} %reduce_sum.30, bf16[3072,3584]{1,0:T(8,128)(2,1)} %all-gather.7.cloned.1.call-done), kind=kOutput, calls=%fused_computation | convolution fusion | flops 39479279616 | bytes 84410368 | tf_op jit(solution)/shard_map/dot_general | solution.py:40
  837.8 0.0 all-gather.13.cloned.1.call-done
  837.8 35.8 %convolution_bitcast_fusion = f32[2048,3584]{0,1:T(8,128)} fusion(bf16[1792,2048]{1,0:T(8,128)(2,1)} %all-gather.13.cloned.1.call-done, f32[3584,1792]{0,1:T(8,128)} %bitcast_add_fusion), kind=kOutput, calls=%fused_computation.1 | convolution fusion | flops 26313097216 | bytes 62390272 | tf_op jit(solution)/shard_map/dot_general | solution.py:54
  873.5 0.0 reduce-scatter.5.cloned.1.call-update
  873.6 1.4 copy.11
  874.9 23.7 %all-gather.11.cloned.1.call-done = bf16[3072,768]{1,0:T(8,128)(2,1)} async-done(((bf16[384,768]{1,0:T(8,128)(2,1)}), bf16[3072,768]{1,0:T(8,128)(2,1)}) %all-gather.11.cloned.1.call-update) | async-done | bytes 4718608 | tf_op jit(solution)/shard_map/all_gather | solution.py:48
  898.6 24.5 %all-gather.9.cloned.1.call-done = bf16[384,3072]{0,1:T(8,128)(2,1)} async-done(((bf16[384,768]{0,1:T(8,128)(2,1)}), bf16[384,3072]{0,1:T(8,128)(2,1)}) %all-gather.9.cloned.1.call-update) | async-done | bytes 2359312 | tf_op jit(solution)/shard_map/all_gather | solution.py:45
  923.1 5.1 multiply_reduce_fusion.1
  928.2 22.3 %psum.14 = f32[768]{0:T(1024)S(1)} all-reduce(f32[768]{0:T(1024)S(1)} %get-tuple-element.10), channel_id=1, replica_groups=mesh['row'=8,'col'=4] {'row'}, use_global_device_ids=true, to_apply=%region_3.4 | all-reduce | flops 768 | bytes 6144 | tf_op jit(solution)/shard_map/psum | solution.py:63
  950.5 1.1 broadcast_multiply_fusion
  951.6 27.4 %copy.12 = f32[3584,1792]{1,0:T(8,128)} copy(f32[3584,1792]{0,1:T(8,128)} %bitcast_add_fusion) | data formatting | bytes 51380224
  979.1 412.4 %reduce-scatter.5.cloned.1.call-done = f32[256,3584]{0,1:T(8,128)} async-done(((f32[2048,3584]{0,1:T(8,128)}), f32[256,3584]{0,1:T(8,128)}) %reduce-scatter.5.cloned.1.call-update) | async-done | bytes 3670032 | tf_op jit(solution)/shard_map/reduce_scatter | solution.py:53
  1391.5 2.5 multiply_reduce_fusion
  1394.0 6.5 psum.15
  1400.5 4.1 multiply_bitcast_fusion
  (2 shorter events, 0.0 us)
Async XLA Ops:
  7.2 426.5 %all-gather.7.cloned.1.call-start = ((), (), s32[]{:S(2)}) async-start(), calls=%async_computation.2 | async-start | bytes 24772608 | tf_op jit(solution)/shard_map/all_gather | solution.py:24
  7.9 492.0 %reduce-scatter.3.cloned.1.call-start = ((), (), s32[]{:S(2)}) async-start(), calls=%async_computation.3 | async-start | bytes 5898240 | tf_op jit(solution)/shard_map/reduce_scatter | solution.py:25
  451.8 311.7 %all-gather.15.cloned.1.call-start = ((), (), s32[]{:S(2)}) async-start(), calls=%async_computation.8 | async-start | bytes 55050240 | tf_op jit(solution)/shard_map/all_gather | solution.py:11
  462.8 374.9 %all-gather.13.cloned.1.call-start = ((), (), s32[]{:S(2)}) async-start(), calls=%async_computation.6 | async-start | bytes 9175040 | tf_op jit(solution)/shard_map/all_gather | solution.py:52
  463.4 435.2 %all-gather.11.cloned.1.call-start = ((), (), s32[]{:S(2)}) async-start(), calls=%async_computation.5 | async-start | bytes 5308416 | tf_op jit(solution)/shard_map/all_gather | solution.py:48
  464.0 27.2 %copy-start = (f32[384,768]{1,0:T(8,128)S(1)}, f32[384,768]{1,0:T(8,128)}, u32[]{:S(2)}) copy-start(f32[384,768]{1,0:T(8,128)} %param.6) | copy-start | bytes 3538948
  464.0 459.1 %all-gather.9.cloned.1.call-start = ((), (), s32[]{:S(2)}) async-start(), calls=%async_computation.4 | async-start | bytes 2949120 | tf_op jit(solution)/shard_map/all_gather | solution.py:45
  502.2 889.3 %reduce-scatter.5.cloned.1.call-start = ((), (), s32[]{:S(2)}) async-start(), calls=%async_computation.7 | async-start | bytes 33030144 | tf_op jit(solution)/shard_map/reduce_scatter | solution.py:53
Sparse Core Ops, SparseCore 0:
  9.5 424.0 all-gather.6
  451.9 47.9 reduce-scatter.2
  501.5 261.9 all-gather.14
  764.9 52.2 all-gather.12
  819.3 79.3 all-gather.10
  900.6 22.4 all-gather.8
  927.0 464.4 reduce-scatter.4
